TPU v7x, 32 devices: a whole 2x2x4 slice. The times are simulated.
32 devices in a mesh: data: 32 (over z, y, x, core).
Axes of the slice: x: 2, y: 2, z: 4, core: 2. Of those that a mesh axis runs over, the one named last changes fastest.
Arguments:
- tokens: bfloat16 [262144, 384], P('data')
- out_grad: bfloat16 [262144, 384], P('data')
- w_up: bfloat16 [2, 384, 1536], replicated
- w_down: bfloat16 [2, 1536, 384], replicated
- a_up_old: float32 [2, 384, 384], replicated
- s_up_old: float32 [2, 1536, 1536], replicated
- a_down_old: float32 [2, 1536, 1536], replicated
- s_down_old: float32 [2, 384, 384], replicated
- a_up_inv: float32 [2, 384, 384], replicated
- s_up_inv: float32 [2, 1536, 1536], replicated
- a_down_inv: float32 [2, 1536, 1536], replicated
- s_down_inv: float32 [2, 384, 384], replicated
- factor_decay: float32 [], replicated
Outputs:
- output 1: float32 [2, 384, 1536], replicated
- output 2: float32 [2, 1536, 384], replicated
- output 3: float32 [2, 384, 384], replicated
- output 4: float32 [2, 1536, 1536], replicated
- output 5: float32 [2, 1536, 1536], replicated
- output 6: float32 [2, 384, 384], replicated
All inputs are finite; a program needn't handle non-finite values.
Results may differ from a plain program's by a relative error of at most 0.00153868.
Values are sent between devices in bfloat16 or wider.
A program may use at most 1 GiB of HBM per device.

v0:
```python
import jax
import jax.numpy as jnp
from jax import lax
from jax.sharding import PartitionSpec as P, NamedSharding


def gelu_fn(pre_act):
    return jax.nn.gelu(pre_act, approximate=True)


def cross_sum(left, right):
    return jnp.einsum("ti,tj->ij", left, right, preferred_element_type=jnp.float32)


def stacked_sums(left_list, right_list, batch_total):
    return jnp.stack([cross_sum(left, right) for left, right in zip(left_list, right_list)]) / batch_total


def precise_chain(left, middle, right):
    inner_prod = jnp.einsum("bij,bjk->bik", left, middle, precision=lax.Precision.HIGHEST,
                            preferred_element_type=jnp.float32)
    return jnp.einsum("bij,bjk->bik", inner_prod, right, precision=lax.Precision.HIGHEST,
                      preferred_element_type=jnp.float32)


def forward_backward(tok_rows, grad_rows, w_up, w_down):
    block_count = w_up.shape[0]
    layer_ins = []
    pre_ups = []
    hiddens = []
    layer_in = tok_rows
    for block_idx in range(block_count):
        pre_up = jnp.dot(layer_in, w_up[block_idx], preferred_element_type=jnp.float32).astype(jnp.bfloat16)
        hidden = gelu_fn(pre_up.astype(jnp.float32)).astype(jnp.bfloat16)
        layer_ins.append(layer_in)
        pre_ups.append(pre_up)
        hiddens.append(hidden)
        if block_idx + 1 < block_count:
            layer_in = jnp.dot(hidden, w_down[block_idx], preferred_element_type=jnp.float32).astype(jnp.bfloat16)
    grad_ups = [None] * block_count
    grad_downs = [None] * block_count
    grad_down = grad_rows
    for block_idx in reversed(range(block_count)):
        grad_downs[block_idx] = grad_down
        d_hidden = jnp.einsum("tj,ij->ti", grad_down, w_down[block_idx],
                              preferred_element_type=jnp.float32).astype(jnp.bfloat16)
        gelu_back = jax.vjp(gelu_fn, pre_ups[block_idx].astype(jnp.float32))[1]
        grad_up = gelu_back(d_hidden.astype(jnp.float32))[0].astype(jnp.bfloat16)
        grad_ups[block_idx] = grad_up
        if block_idx > 0:
            grad_down = jnp.einsum("tj,ij->ti", grad_up, w_up[block_idx],
                                   preferred_element_type=jnp.float32).astype(jnp.bfloat16)
    return layer_ins, hiddens, grad_ups, grad_downs


def update_outputs(dw_up, dw_down, fresh_factors, old_factors, inverses, factor_decay):
    new_factors = tuple(factor_decay * old_part + (1.0 - factor_decay) * new_part
                        for old_part, new_part in zip(old_factors, fresh_factors))
    precond_up = precise_chain(inverses[0], dw_up, inverses[1])
    precond_down = precise_chain(inverses[2], dw_down, inverses[3])
    return (precond_up, precond_down) + new_factors


def solution(mesh):
    axis_size = mesh.shape["data"]

    def local_step(tok_rows, grad_rows, w_up, w_down, a_up_old, s_up_old, a_down_old, s_down_old,
                   a_up_inv, s_up_inv, a_down_inv, s_down_inv, factor_decay):
        batch_total = tok_rows.shape[0] * axis_size
        layer_ins, hiddens, grad_ups, grad_downs = forward_backward(tok_rows, grad_rows, w_up, w_down)
        local_parts = (stacked_sums(layer_ins, grad_ups, batch_total),
                       stacked_sums(hiddens, grad_downs, batch_total),
                       stacked_sums(layer_ins, layer_ins, batch_total),
                       stacked_sums(grad_ups, grad_ups, batch_total),
                       stacked_sums(hiddens, hiddens, batch_total),
                       stacked_sums(grad_downs, grad_downs, batch_total))
        totals = [lax.psum(part, "data") for part in local_parts]
        return update_outputs(totals[0], totals[1], tuple(totals[2:]),
                              (a_up_old, s_up_old, a_down_old, s_down_old),
                              (a_up_inv, s_up_inv, a_down_inv, s_down_inv), factor_decay)

    batch_spec = P("data", None)
    replicated = P()
    return jax.shard_map(local_step, mesh=mesh, in_specs=(batch_spec, batch_spec) + (replicated,) * 11,
                         out_specs=(replicated,) * 6, check_vma=False)
```

profile of v0, /device:TPU:0, one launch (start us, length us, event | category | flops | bytes accessed | tf_op | source)
XLA Modules:
  0.0 1414.9 jit_solution(11728408231658972904)
XLA Ops:
  7.2 9.0 convolution_bitcast_fusion.11
  16.2 33.3 %fusion.13 = (bf16[8192,1536]{1,0:T(8,128)(2,1)}, bf16[8192,1536]{1,0:T(8,128)(2,1)}) fusion(bf16[8192,384]{1,0:T(8,128)(2,1)} %param.13, bf16[2,384,1536]{2,1,0:T(8,128)(2,1)S(1)} %copy-done.16), kind=kOutput, calls=%fused_computation.25 | convolution fusion | flops 9802088448 | bytes 57802752 | tf_op jit(solution)/shard_map/dot_general | solution.py:33
  49.5 52.3 %convolution_bitcast_fusion.1 = f32[1,1536,1536]{2,1,0:T(8,128)} fusion(bf16[8192,1536]{1,0:T(8,128)(2,1)} %get-tuple-element.12), kind=kOutput, calls=%fused_computation.45 | convolution fusion | flops 38654705664 | bytes 34603008 | tf_op jit(solution)/shard_map/ti,tj->ij/dot_general | solution.py:12
  101.9 18.2 %convolution_convert_fusion.5 = bf16[8192,384]{1,0:T(8,128)(2,1)S(1)} fusion(bf16[8192,1536]{1,0:T(8,128)(2,1)} %get-tuple-element.12, bf16[2,1536,384]{2,1,0:T(8,128)(2,1)S(1)} %copy-done.18), kind=kOutput, calls=%fused_computation.43 | convolution fusion | flops 9666822144 | bytes 32636928 | tf_op jit(solution)/shard_map/dot_general | solution.py:39
  127.0 19.9 %convolution_convert_fusion.1 = bf16[8192,1536]{1,0:T(8,128)(2,1)} fusion(bf16[8192,384]{1,0:T(8,128)(2,1)} %copy-done.1, bf16[2,384,1536]{2,1,0:T(8,128)(2,1)S(1)} %copy-done.16), kind=kOutput, calls=%fused_computation.35 | convolution fusion | flops 9676259328 | bytes 32636928 | tf_op jit(solution)/shard_map/dot_general | solution.py:33
  147.0 9.0 convolution_bitcast_fusion.8
  156.0 26.8 %convolution_bitcast_fusion.5 = f32[1,1536,384]{2,1,0:T(8,128)} fusion(bf16[8192,384]{1,0:T(8,128)(2,1)} %param.14, bf16[8192,1536]{1,0:T(8,128)(2,1)} %convolution_convert_fusion.1), kind=kOutput, calls=%fused_computation.51 | convolution fusion | flops 9789505536 | bytes 33816576 | tf_op jit(solution)/shard_map/ti,tj->ij/dot_general | solution.py:12
  182.8 47.9 %fusion.4 = bf16[8192,1536]{1,0:T(8,128)(2,1)} fusion(bf16[8192,1536]{1,0:T(8,128)(2,1)} %convolution_convert_fusion.1, bf16[8192,384]{1,0:T(8,128)(2,1)S(1)} %bitcast.83, bf16[2,1536,384]{2,1,0:T(8,128)(2,1)S(1)} %copy-done.19), kind=kOutput, calls=%fused_computation.16 | convolution fusion | flops 9953083392 | bytes 57802752 | tf_op jit(solution)/shard_map/tj,ij->ti/dot_general | solution.py:45
  230.7 26.2 %fusion.79 = bf16[8192,1536]{1,0:T(8,128)(2,1)} fusion(bf16[8192,1536]{1,0:T(8,128)(2,1)} %convolution_convert_fusion.1), kind=kLoop, calls=%fused_computation.33.clone.clone.2 | loop fusion | flops 125829120 | bytes 50331648 | tf_op jit(solution)/shard_map/ti,tj->ij/dot_general | solution.py:12
  256.9 18.0 %convolution_bitcast_fusion.4 = f32[1,384,1536]{1,2,0:T(8,128)} fusion(bf16[8192,384]{1,0:T(8,128)(2,1)S(1)} %copy-done.2, bf16[8192,1536]{1,0:T(8,128)(2,1)} %fusion.4), kind=kOutput, calls=%fused_computation.50 | convolution fusion | flops 9663676416 | bytes 33816576 | tf_op jit(solution)/shard_map/ti,tj->ij/dot_general | solution.py:12
  275.0 18.1 %convolution_convert_fusion.4 = bf16[8192,384]{1,0:T(8,128)(2,1)S(1)} fusion(bf16[8192,1536]{1,0:T(8,128)(2,1)} %fusion.4, bf16[2,384,1536]{2,1,0:T(8,128)(2,1)S(1)} %copy-done.17), kind=kOutput, calls=%fused_computation.42 | convolution fusion | flops 9666822144 | bytes 32636928 | tf_op jit(solution)/shard_map/tj,ij->ti/dot_general | solution.py:51
  293.0 52.3 %convolution_bitcast_fusion.2 = f32[1,1536,1536]{2,1,0:T(8,128)} fusion(bf16[8192,1536]{1,0:T(8,128)(2,1)} %fusion.4), kind=kOutput, calls=%fused_computation.46 | convolution fusion | flops 38654705664 | bytes 34603008 | tf_op jit(solution)/shard_map/ti,tj->ij/dot_general | solution.py:12
  345.3 18.0 %convolution_bitcast_fusion.6 = f32[1,1536,384]{2,1,0:T(8,128)} fusion(bf16[8192,1536]{1,0:T(8,128)(2,1)} %get-tuple-element.12, bf16[8192,384]{1,0:T(8,128)(2,1)S(1)} %convolution_convert_fusion.4), kind=kOutput, calls=%fused_computation.52 | convolution fusion | flops 9663676416 | bytes 33816576 | tf_op jit(solution)/shard_map/ti,tj->ij/dot_general | solution.py:12
  367.6 48.0 %fusion.7 = bf16[8192,1536]{1,0:T(8,128)(2,1)} fusion(bf16[8192,1536]{1,0:T(8,128)(2,1)} %get-tuple-element.13, bf16[8192,384]{1,0:T(8,128)(2,1)S(1)} %convolution_convert_fusion.4, bf16[2,1536,384]{2,1,0:T(8,128)(2,1)S(1)} %copy-done.19), kind=kOutput, calls=%fused_computation.19 | convolution fusion | flops 9953083392 | bytes 57802752 | tf_op jit(solution)/shard_map/tj,ij->ti/dot_general | solution.py:45
  415.7 17.8 %convolution_bitcast_fusion.7 = f32[1,384,1536]{1,2,0:T(8,128)} fusion(bf16[8192,1536]{1,0:T(8,128)(2,1)} %fusion.7, bf16[8192,384]{1,0:T(8,128)(2,1)S(1)} %bitcast.85), kind=kOutput, calls=%fused_computation.53 | convolution fusion | flops 9663676416 | bytes 33816576 | tf_op jit(solution)/shard_map/ti,tj->ij/dot_general | solution.py:12
  433.5 52.3 %convolution_bitcast_fusion.3 = f32[1,1536,1536]{2,1,0:T(8,128)} fusion(bf16[8192,1536]{1,0:T(8,128)(2,1)} %fusion.7), kind=kOutput, calls=%fused_computation.47 | convolution fusion | flops 38654705664 | bytes 34603008 | tf_op jit(solution)/shard_map/ti,tj->ij/dot_general | solution.py:12
  485.7 52.0 %convolution_bitcast_fusion = f32[1,1536,1536]{2,1,0:T(8,128)} fusion(bf16[8192,1536]{1,0:T(8,128)(2,1)} %fusion.79), kind=kOutput, calls=%fused_computation.44 | convolution fusion | flops 38654705664 | bytes 34603008 | tf_op jit(solution)/shard_map/ti,tj->ij/dot_general | solution.py:12
  538.8 17.2 %maximum_multiply_fusion.1 = f32[2,1536,1536]{2,1,0:T(8,128)} fusion(f32[1,1536,1536]{2,1,0:T(8,128)} %convolution_bitcast_fusion, f32[1,1536,1536]{2,1,0:T(8,128)} %convolution_bitcast_fusion.1), kind=kLoop, calls=%fused_computation.39 | loop fusion | flops 9437184 | bytes 37748736 | tf_op jit(solution)/shard_map/div | solution.py:16
  572.2 714.3 %all-reduce.3.cloned.1.call-done = (f32[2,384,1536]{1,2,0:T(8,128)}, f32[2,1536,384]{2,1,0:T(8,128)}, f32[2,384,384]{2,1,0:T(8,128)}, f32[2,1536,1536]{2,1,0:T(8...) async-done(((f32[2,384,1536]{1,2,0:T(8,128)}, f32[2,1536,384]{2,1,0:T(8,128)}, f32[2,384,384]{2,1,0:T(8,128)}, f32[2,1536,1536]{2,1,0:T(8,128)}, ...) | async-done | bytes 49545232 | tf_op jit(solution)/shard_map/psum | solution.py:77
  1286.6 9.7 fusion.36
  1296.4 27.5 %fusion.37 = f32[2,384,1536]{2,1,0:T(8,128)} fusion(f32[2,1536,384]{1,2,0:T(8,128)S(1)} %fusion.36, f32[2,1536,1536]{2,1,0:T(8,128)} %param.22), kind=kOutput, calls=%fused_computation.75 | convolution fusion | flops 21743271936 | bytes 28311552 | tf_op jit(solution)/shard_map/bij,bjk->bik/dot_general | solution.py:22
  1324.0 31.5 %fusion.38 = f32[2,384,1536]{1,2,0:T(8,128)S(1)} fusion(f32[2,1536,384]{2,1,0:T(8,128)S(1)} %bitcast.89, f32[2,1536,1536]{2,1,0:T(8,128)S(1)} %bitcast.87), kind=kOutput, calls=%fused_computation.76 | convolution fusion | flops 21743271936 | bytes 28311552 | tf_op jit(solution)/shard_map/bij,bjk->bik/dot_general | solution.py:20
  1355.5 10.5 fusion.39
  1369.3 38.5 %multiply_add_fusion = (f32[2,1536,1536]{2,1,0:T(8,128)}, f32[2,1536,1536]{2,1,0:T(8,128)}) fusion(f32[2,1536,1536]{2,1,0:T(8,128)} %get-tuple-element.10, f32[2,1536,1536]{2,1,0:T(8,128)} %param.19, f32[]{:T(128)S(6)} %sub.14, f32[]{:T(128)S(6)} %copy.27, f32[2,1536,1536]{2,1,0:T(8,128)} %get-tuple-element.9, f32[2,1536,1536]{2,1,0:T(8,128)} %param.18), kind=kLoop, calls=%fused_computation.40 | loop fusion | flops 28311552 | bytes 113246216 | tf_op jit(solution)/shard_map/add | solution.py:57
  (76 shorter events, 31.3 us)
Async XLA Ops:
  7.2 1279.4 %copy-start = (f32[2,384,384]{2,1,0:T(8,128)S(1)}, f32[2,384,384]{2,1,0:T(8,128)}, u32[]{:S(2)}) copy-start(f32[2,384,384]{2,1,0:T(8,128)} %param.21) | copy-start | bytes 3538948
  7.2 1279.4 %all-reduce.3.cloned.1.call-start = ((), (), s32[]{:S(2)}) async-start(), calls=%async_computation | async-start | bytes 99090432 | tf_op jit(solution)/shard_map/psum | solution.py:77
  49.5 52.3 %copy-start.18 = (bf16[2,1536,384]{2,1,0:T(8,128)(2,1)S(1)}, bf16[2,1536,384]{2,1,0:T(8,128)(2,1)}, u32[]{:S(2)}) copy-start(bf16[2,1536,384]{2,1,0:T(8,128)(2,1)} %param.16) | copy-start | bytes 7077892
  147.0 35.8 %slice-start = ((s8[6291456]{0:T(1024)(128)(4,1)}), s8[4194304]{0:T(1024)(128)(4,1)S(1)}, s32[]{:S(2)}) async-start(s8[6291456]{0:T(1024)(128)(4,1)} %bitcast.82), calls=%async_computation.1 | async-start | bytes 8388608
  155.9 26.8 %slice-start.1 = ((s8[6291456]{0:T(1024)(128)(4,1)}), s8[2097152]{0:T(1024)(128)(4,1)S(1)}, s32[]{:S(2)}) async-start(s8[6291456]{0:T(1024)(128)(4,1)} %bitcast.82), calls=%async_computation.2 | async-start | bytes 4194304
  156.0 26.8 %copy-start.19 = (bf16[2,1536,384]{2,1,0:T(8,128)(2,1)S(1)}, bf16[2,1536,384]{2,1,0:T(8,128)(2,1)}, u32[]{:S(2)}) copy-start(bf16[2,1536,384]{2,1,0:T(8,128)(2,1)} %param.16) | copy-start | bytes 7077892
  230.7 26.2 %copy-start.2 = (bf16[8192,384]{1,0:T(8,128)(2,1)S(1)}, bf16[8192,384]{1,0:T(8,128)(2,1)}, u32[]{:S(2)}) copy-start(bf16[8192,384]{1,0:T(8,128)(2,1)} %copy-done.1) | copy-start | bytes 18874372
  363.4 52.3 %slice-start.2 = ((s8[6291456]{0:T(1024)(128)(4,1)}), s8[4194304]{0:T(1024)(128)(4,1)S(1)}, s32[]{:S(2)}) async-start(s8[6291456]{0:T(1024)(128)(4,1)} %bitcast.84), calls=%async_computation.3 | async-start | bytes 8388608
  367.6 48.0 %slice-start.3 = ((s8[6291456]{0:T(1024)(128)(4,1)}), s8[2097152]{0:T(1024)(128)(4,1)S(1)}, s32[]{:S(2)}) async-start(s8[6291456]{0:T(1024)(128)(4,1)} %bitcast.84), calls=%async_computation.4 | async-start | bytes 4194304
  485.7 52.0 %copy-start.5 = (f32[1,384,384]{2,1,0:T(8,128)S(1)}, f32[1,384,384]{2,1,0:T(8,128)}, u32[]{:S(2)}) copy-start(f32[1,384,384]{2,1,0:T(8,128)} %convolution_bitcast_fusion.11) | copy-start | bytes 1769476
  485.7 52.0 %copy-start.7 = (f32[1,384,384]{2,1,0:T(8,128)S(1)}, f32[1,384,384]{2,1,0:T(8,128)}, u32[]{:S(2)}) copy-start(f32[1,384,384]{2,1,0:T(8,128)} %convolution_bitcast_fusion.10) | copy-start | bytes 1769476
  538.8 18.3 %copy-start.11 = (f32[1,1536,384]{2,1,0:T(8,128)S(1)}, f32[1,1536,384]{2,1,0:T(8,128)}, u32[]{:S(2)}) copy-start(f32[1,1536,384]{2,1,0:T(8,128)} %convolution_bitcast_fusion.6) | copy-start | bytes 7077892
  538.8 21.0 %copy-start.3 = (f32[1,1536,1536]{2,1,0:T(8,128)S(1)}, f32[1,1536,1536]{2,1,0:T(8,128)}, u32[]{:S(2)}) copy-start(f32[1,1536,1536]{2,1,0:T(8,128)} %convolution_bitcast_fusion.2) | copy-start | bytes 28311556
  538.8 22.6 %copy-start.4 = (f32[1,1536,1536]{2,1,0:T(8,128)S(1)}, f32[1,1536,1536]{2,1,0:T(8,128)}, u32[]{:S(2)}) copy-start(f32[1,1536,1536]{2,1,0:T(8,128)} %convolution_bitcast_fusion.3) | copy-start | bytes 28311556
  1286.6 37.3 %slice-start.4 = ((s8[18874368]{0:T(1024)(128)(4,1)}), s8[4194304]{0:T(1024)(128)(4,1)S(1)}, s32[]{:S(2)}) async-start(s8[18874368]{0:T(1024)(128)(4,1)} %bitcast.86), calls=%async_computation.5 | async-start | bytes 8388608
  1286.6 37.3 %slice-start.5 = ((s8[18874368]{0:T(1024)(128)(4,1)}), s8[4194304]{0:T(1024)(128)(4,1)S(1)}, s32[]{:S(2)}) async-start(s8[18874368]{0:T(1024)(128)(4,1)} %bitcast.86), calls=%async_computation.6 | async-start | bytes 8388608
  1286.6 37.3 %slice-start.9 = ((s8[4718592]{0:T(1024)(128)(4,1)}), s8[4194304]{0:T(1024)(128)(4,1)S(1)}, s32[]{:S(2)}) async-start(s8[4718592]{0:T(1024)(128)(4,1)} %bitcast.88), calls=%async_computation.10 | async-start | bytes 8388608
  1296.3 27.6 %slice-start.6 = ((s8[18874368]{0:T(1024)(128)(4,1)}), s8[4194304]{0:T(1024)(128)(4,1)S(1)}, s32[]{:S(2)}) async-start(s8[18874368]{0:T(1024)(128)(4,1)} %bitcast.86), calls=%async_computation.7 | async-start | bytes 8388608
  1296.3 27.6 %slice-start.7 = ((s8[18874368]{0:T(1024)(128)(4,1)}), s8[4194304]{0:T(1024)(128)(4,1)S(1)}, s32[]{:S(2)}) async-start(s8[18874368]{0:T(1024)(128)(4,1)} %bitcast.86), calls=%async_computation.8 | async-start | bytes 8388608
  1296.3 27.6 %slice-start.8 = ((s8[18874368]{0:T(1024)(128)(4,1)}), s8[2097152]{0:T(1024)(128)(4,1)S(1)}, s32[]{:S(2)}) async-start(s8[18874368]{0:T(1024)(128)(4,1)} %bitcast.86), calls=%async_computation.9 | async-start | bytes 4194304
  1296.4 27.6 %slice-start.10 = ((s8[4718592]{0:T(1024)(128)(4,1)}), s8[524288]{0:T(1024)(128)(4,1)S(1)}, s32[]{:S(2)}) async-start(s8[4718592]{0:T(1024)(128)(4,1)} %bitcast.88), calls=%async_computation.11 | async-start | bytes 1048576
  1323.9 31.5 %copy-start.13 = (f32[2,384,384]{2,1,0:T(8,128)S(1)}, f32[2,384,384]{2,1,0:T(8,128)}, u32[]{:S(2)}) copy-start(f32[2,384,384]{2,1,0:T(8,128)} %param.24) | copy-start | bytes 3538948
  1324.0 42.0 %copy-start.14 = (f32[2,384,384]{2,1,0:T(8,128)S(1)}, f32[2,384,384]{2,1,0:T(8,128)}, u32[]{:S(2)}) copy-start(f32[2,384,384]{2,1,0:T(8,128)} %param.20) | copy-start | bytes 3538948
  1324.0 42.0 %copy-start.15 = (f32[2,384,384]{2,1,0:T(8,128)S(1)}, f32[2,384,384]{2,1,0:T(8,128)}, u32[]{:S(2)}) copy-start(f32[2,384,384]{2,1,0:T(8,128)} %param.17) | copy-start | bytes 3538948
  (8 other events, 97.8 us)
Sparse Core Ops, SparseCore 0:
  571.7 714.8 all-reduce.2
where the time goes:
time: 1420 us; the launch traced here: 1410 us
  waiting for transfers between devices  714 us (50%)
  matrix products  581 us (41%)
  other arithmetic  100 us (7%)
  between operations  15.2 us (1%)
    psum x1, waiting for transfers between devices, local_step(): totals = [lax.psum(part, 'data') for part in local_parts]  714 us
    dot_general x12, matrix products, cross_sum(): jnp.einsum('ti,tj->ij', left, right, preferred_element_type=jnp.float32)  316 us
    dot_general x2, matrix products, forward_backward(): jnp.einsum('tj,ij->ti', grad_down, w_down[block_idx], preferred_element_t...  95.9 us
    dot_general x2, matrix products, forward_backward(): jnp.dot(layer_in, w_up[block_idx], preferred_element_type=jnp.float32)  53.3 us
    add x2, other arithmetic, update_outputs(): factor_decay * old_part + (1.0 - factor_decay) * new_part  41.8 us
    dot_general x2, matrix products, precise_chain(): jnp.einsum('bij,bjk->bik', left, middle, precision=lax.Precision.HIGHEST,...  41.2 us
    dot_general x2, matrix products, precise_chain(): jnp.einsum('bij,bjk->bik', inner_prod, right, precision=lax.Precision.HIG...  38 us
    div x6, other arithmetic, stacked_sums(): jnp.stack([cross_sum(left, right) for left, right in zip(left_list, right...  32.2 us
  transfers between devices with their start and end apart: 1, of which 1 were waited for; matrix products, arithmetic and copies ran while one was open for 0% of the time, Pallas kernels for 0%

commit v1 on v0

v1 whole, which is shorter than its diff:
```python
import functools

import jax
import jax.numpy as jnp
from jax import lax
from jax.experimental import pallas as pl
from jax.experimental.pallas import tpu as pltpu
from jax.sharding import PartitionSpec as P

bf16 = jnp.bfloat16
f32 = jnp.float32
MESH = pl.DeviceIdType.MESH
ORDER_X = (1, 2, 3, 4)
ORDER_Y = (2, 1, 3, 4)
ORDER_Z = (3, 4, 1, 2)


D, FF, B = 384, 1536, 256
NB = FF // B
TRI = sum((j + 1) * B for j in range(NB))
NN = (((1,), (0,)), ((), ()))
NT = (((1,), (1,)), ((), ()))
TN = (((0,), (0,)), ((), ()))
TT = (((0,), (1,)), ((), ()))
GELU_K = 0.7978845608028654
GELU_C = 0.044715 * GELU_K
MIB = 1 << 20


def mm(left, right, dims):
    return lax.dot_general(left, right, dims, preferred_element_type=f32)


def half_sig(pre):
    cubic = GELU_C * (pre * pre)
    return 0.5 * jnp.tanh(pre * (cubic + GELU_K)) + 0.5, cubic


def gelu_back(pre, sig, cubic):
    hid = pre * sig
    return hid, sig + (hid * (1.0 - sig)) * (6.0 * cubic + 2.0 * GELU_K)


def add_tri(acc, mat):
    off = 0
    for j in range(NB):
        rows = (j + 1) * B
        acc[off:off + rows, :] += mm(mat[:rows, :], mat[j * B:rows, :], NT)
        off += rows


def add_small_tn(acc, rows):
    acc[0] += mm(rows[:, 0:128], rows[...], TN)
    acc[1, :, 0:256] += mm(rows[:, 128:256], rows[:, 128:384], TN)
    acc[1, :, 256:384] += mm(rows[:, 256:384], rows[:, 256:384], TN)


def add_small_nt(acc, cols):
    acc[0] += mm(cols[0:128, :], cols[...], NT)
    acc[1, :, 0:256] += mm(cols[128:256, :], cols[128:384, :], NT)
    acc[1, :, 256:384] += mm(cols[256:384, :], cols[256:384, :], NT)


def zero_first(accs):
    @pl.when(pl.program_id(0) == 0)
    def _():
        for acc in accs:
            acc[...] = jnp.zeros_like(acc)


def my_bits():
    me = lax.axis_index("data")
    return me, [(me // (1 << d)) % 2 for d in range(5)]


class Chain:
    def __init__(self, row0, rows, cols, order):
        self.row0, self.rows, self.cols, self.order = row0, rows, cols, order


def entry_barrier():
    me, bits = my_bits()
    barrier = pltpu.get_barrier_semaphore()
    for d in range(5):
        pl.semaphore_signal(barrier, inc=1, device_id=(me + (1 - 2 * bits[d]) * (1 << d),), device_id_type=MESH)
    pl.semaphore_wait(barrier, 5)


class Job:
    def __init__(self, kind, chain, src=None, shard=None, shard_row=0, dst=None, start=0.0):
        self.kind, self.chain, self.start = kind, chain, start
        self.src, self.shard, self.shard_row, self.dst = src, shard, shard_row, dst
        self.n_events = {"rs": 7, "ag": 7, "ar": 11, "fan": 6}[kind]

    def scratch(self):
        ch = self.chain
        out = []
        if self.kind in ("rs", "ar"):
            out += [pltpu.VMEM((ch.rows, ch.cols), f32), pltpu.VMEM((ch.rows * 31 // 16, ch.cols), f32)]
        elif self.kind == "ag":
            out += [pltpu.VMEM((ch.rows // 16, ch.cols), f32)]
        n = 5 if self.kind != "ar" else 10
        out += [pltpu.SemaphoreType.DMA((2,)), pltpu.SemaphoreType.DMA((n,)), pltpu.SemaphoreType.DMA((n,))]
        return out

    def messages(self):
        ch = self.chain
        size = ch.rows * ch.cols * 4
        rs = [(size, 0)] + [(size >> (k + 1), ch.order[k]) for k in range(4)]
        ag = [(size >> (k + 1), ch.order[k]) for k in (3, 2, 1, 0)] + [(size, 0)]
        return {"rs": rs + [(0, None)], "ag": [(0, None)] + ag, "fan": ag, "ar": rs + ag + [(0, None)]}[self.kind]

    def bind(self, refs, scr):
        ch = self.chain
        rows, half = ch.rows, ch.rows // 2
        me, bits = my_bits()
        core = bits[0]
        peers = [me + (1 - 2 * bits[d]) * (1 << d) for d in range(5)]
        offs, lens = [0], [rows]
        for d in ch.order:
            lens.append(lens[-1] // 2)
            offs.append(offs[-1] + bits[d] * lens[-1])
        starts = [0, rows, rows * 3 // 2, rows * 7 // 4, rows * 15 // 8]
        al = lambda v: pl.multiple_of(v, 8)
        if self.kind == "ag":
            buf, sem_l, sem_s, sem_r = scr
            sem0 = 0
        elif self.kind == "fan":
            sem_l, sem_s, sem_r = scr
            sem0 = 0
        else:
            work, recv, sem_l, sem_s, sem_r = scr
            sem0 = 5
        src = refs.get(self.src)
        dst = refs.get(self.dst)
        shard = refs.get(self.shard)

        def remote(a, b, i, d):
            return pltpu.make_async_remote_copy(src_ref=a, dst_ref=b, send_sem=sem_s.at[i], recv_sem=sem_r.at[i],
                                                device_id=(peers[d],), device_id_type=MESH)

        events = []
        if self.kind in ("rs", "ar"):
            load = pltpu.make_async_copy(src.at[core, pl.ds(ch.row0, rows), :], work, sem_l.at[0])
            first = remote(src.at[1 - core, pl.ds(ch.row0, rows), :], recv.at[pl.ds(0, rows), :], 0, 0)
            sends = [first]
            for k in range(4):
                gone = al(offs[k] + (1 - bits[ch.order[k]]) * lens[k + 1])
                sends.append(remote(work.at[pl.ds(gone, lens[k + 1]), :], recv.at[pl.ds(starts[k + 1], lens[k + 1]), :],
                                    k + 1, ch.order[k]))

            def add(at, frm, count):
                for q in range(0, count, 64):
                    step = min(count - q, 64)
                    a = al(at + q)
                    b = al(frm + q)
                    work[pl.ds(a, step), :] = work[pl.ds(a, step), :] + recv[pl.ds(b, step), :]

            def begin():
                load.start()
                first.start()

            def fold(k):
                def run():
                    if k == 0:
                        load.wait()
                    sends[k].wait_recv()
                    if k < 4:
                        n = lens[k + 1]
                        b = bits[ch.order[k]]
                        add(offs[k] + (1 - b) * n, starts[k] + (1 - b) * n, n)
                        sends[k + 1].start()
                        add(offs[k] + b * n, starts[k] + b * n, n)
                    else:
                        add(offs[4], starts[4], lens[4])
                        tail()
                return run

            events += [begin] + [fold(k) for k in range(5)]
            final = work.at[pl.ds(al(offs[4]), lens[4]), :]
            if self.kind == "rs":
                out = pltpu.make_async_copy(final, shard.at[pl.ds(self.shard_row, lens[4]), :], sem_l.at[1])

                def tail():
                    out.start()

                def end():
                    out.wait()
                    for s in sends:
                        s.wait_send()

                events.append(end)
                return events
        elif self.kind == "fan":
            final = self.after.prod.at[pl.ds(self.row, lens[4]), :]
        else:
            final = buf
            load = pltpu.make_async_copy(shard.at[pl.ds(self.shard_row, lens[4]), :], buf, sem_l.at[0])

            def begin():
                load.start()

            events.append(begin)

        place = pltpu.make_async_copy(final, dst.at[core, pl.ds(al(ch.row0 + offs[4]), lens[4]), :], sem_l.at[1])
        outs = [remote(final, dst.at[core, pl.ds(al(ch.row0 + offs[4]), lens[4]), :], sem0, ch.order[3])]
        for i, k in enumerate((3, 2, 1)):
            part = dst.at[core, pl.ds(al(ch.row0 + offs[k]), lens[k]), :]
            outs.append(remote(part, part, sem0 + 1 + i, ch.order[k - 1]))
        part = dst.at[core, pl.ds(ch.row0, rows), :]
        outs.append(remote(part, part, sem0 + 4, 0))

        def tail():
            place.start()
            outs[0].start()

        if self.kind == "ag":
            def second():
                load.wait()
                tail()
            events.append(second)
        if self.kind == "fan":
            events.append(tail)

        def spread(i):
            def run():
                if i == 1:
                    place.wait()
                outs[i - 1].wait_recv()
                outs[i].start()
            return run

        events += [spread(i) for i in range(1, 5)]

        def end():
            outs[4].wait_recv()
            for s in (sends if self.kind == "ar" else []) + outs:
                s.wait_send()

        events.append(end)
        return events


RATE = {0: 600e3, 1: 44e3, 2: 44e3, 3: 44e3, 4: 22e3}
LINK = {0: 0, 1: 1, 2: 2, 3: 3, 4: 3}


def plan(jobs, ticks, tick_us, lag=2.5):
    free = {}
    state = [[0, 1e9 if getattr(job, "after", None) else job.start] for job in jobs]
    slots = [[] for _ in range(ticks)]
    rest = []

    def fire(j, now):
        e, _ = state[j]
        msgs = jobs[j].messages()
        ready = now
        if e < len(msgs) and msgs[e][1] is not None:
            size, d = msgs[e]
            begin = max(now, free.get(LINK[d], 0.0))
            ready = begin + size / RATE[d]
            free[LINK[d]] = ready
            ready += lag
        elif e + 1 < jobs[j].n_events:
            ready = now + lag
        state[j] = [e + 1, ready]
        if e + 1 == jobs[j].n_events:
            for i, job in enumerate(jobs):
                if getattr(job, "after", None) is jobs[j]:
                    state[i][1] = now

    for t in range(ticks):
        now = t * tick_us
        order = sorted((s[1], j) for j, s in enumerate(state) if s[0] < jobs[j].n_events and s[1] <= now)
        for _, j in order:
            slots[t].append((j, state[j][0]))
            fire(j, now)
    now = ticks * tick_us
    while True:
        todo = sorted((s[1], j) for j, s in enumerate(state) if s[0] < jobs[j].n_events)
        if not todo:
            return slots, rest, now
        ready, j = todo[0]
        now = max(now, ready)
        rest.append((j, state[j][0]))
        fire(j, now)


def stage1(tok, grad, w_up, w_down, pre_out, next_out, tri, small_u, small_q, hid_s, up_s, down_s):
    zero_first((tri, small_u, small_q))

    @pl.when(pl.program_id(0) == 0)
    def _():
        up_s[...] = w_up[0].T
        down_s[...] = w_down[0].T

    pre = mm(up_s[...], tok[...], NT).astype(bf16)
    pre_out[...] = pre
    pre = pre.astype(f32)
    hid_s[...] = (pre * half_sig(pre)[0]).astype(bf16)
    add_tri(tri, hid_s)
    next_out[...] = mm(down_s[...], hid_s[...], NN).astype(bf16)
    add_small_tn(small_u, tok)
    add_small_tn(small_q, grad)


def stage2(u_t, grad, w_up, pre_out, tri, small_u, dwd, hid_s, up_s):
    zero_first((tri, small_u, dwd))

    @pl.when(pl.program_id(0) == 0)
    def _():
        up_s[...] = w_up[0].T

    pre = mm(up_s[...], u_t[...], NN).astype(bf16)
    pre_out[...] = pre
    pre = pre.astype(f32)
    hid_s[...] = (pre * half_sig(pre)[0]).astype(bf16)
    add_small_nt(small_u, u_t)
    add_tri(tri, hid_s)
    dwd[0] += mm(grad[...], hid_s[:FF // 2, :], TT)
    dwd[1] += mm(grad[...], hid_s[FF // 2:, :], TT)


def stage3(pre_in, grad, u_t, w_down, w_up, err_out, tri, dwu, g_s):
    zero_first((tri, dwu))
    d_hid = mm(w_down[0], grad[...], NT).astype(bf16).astype(f32)
    pre = pre_in[...].astype(f32)
    sig, cubic = half_sig(pre)
    g_s[...] = (d_hid * gelu_back(pre, sig, cubic)[1]).astype(bf16)
    add_tri(tri, g_s)
    dwu[0] += mm(u_t[...], g_s[:FF // 2, :], NT)
    dwu[1] += mm(u_t[...], g_s[FF // 2:, :], NT)
    err_out[...] = mm(w_up[0], g_s[...], NN).astype(bf16)


def stage4(pre_in, tok, err_t, w_down, g_out, small_q, dwd, dwu, hid_s):
    zero_first((small_q, dwd, dwu))
    d_hid = mm(w_down[0], err_t[...], NN).astype(bf16).astype(f32)
    pre = pre_in[...].astype(f32)
    sig, cubic = half_sig(pre)
    hid, slope = gelu_back(pre, sig, cubic)
    hid_s[...] = hid.astype(bf16)
    g_out[...] = (d_hid * slope).astype(bf16)
    add_small_nt(small_q, err_t)
    dwd[0] += mm(err_t[...], hid_s[:FF // 2, :], NT)
    dwd[1] += mm(err_t[...], hid_s[FF // 2:, :], NT)
    dwu[0] += mm(tok[...], g_out[:FF // 2, :], TT)
    dwu[1] += mm(tok[...], g_out[FF // 2:, :], TT)


def stage5(g_in, tri):
    zero_first((tri,))
    add_tri(tri, g_in)


SMALL = (2, 128, 384)
WIDE = (2, 384, 768)
TRI_SHAPE = (2, TRI // 2, B)
TRI_CHAINS = [Chain(0, 640, B, ORDER_X), Chain(640, 640, B, ORDER_Y), Chain(1280, 512, B, ORDER_X),
              Chain(1792, 512, B, ORDER_Y), Chain(2304, 384, B, ORDER_Z)]
WIDE_CHAINS = [Chain(0, 128, 768, ORDER_X), Chain(128, 128, 768, ORDER_Y), Chain(256, 128, 768, ORDER_Z)]
SMALL_CHAINS = [Chain(0, 128, 384, ORDER_Y)]
FORMS = {"tri": (TRI_SHAPE, TRI_CHAINS), "wide": (WIDE, WIDE_CHAINS), "small": (SMALL, SMALL_CHAINS)}


def form_jobs(kind, form, name):
    shape, chains = FORMS[form]
    jobs, row = [], 0
    for chain in chains:
        jobs.append(Job(kind, chain, src=name + ":src", shard=name + ":shard", shard_row=row, dst=name + ":dst"))
        row += chain.rows // 16
    return jobs


class First:
    n_events = 2
    kind = "first"
    start = 0.0

    def __init__(self, name):
        self.name = name

    def scratch(self):
        return [pltpu.VMEM((24, 768), f32), pltpu.VMEM((24, 768), f32), pltpu.VMEM((24, 768), f32),
                pltpu.VMEM((FF, 768), f32), pltpu.SemaphoreType.DMA((2,)), pltpu.SemaphoreType.DMA((1,)),
                pltpu.SemaphoreType.DMA((1,))]

    def messages(self):
        return [(24 * 768 * 4 + 4000000, 0), (0, None)]

    def bind(self, refs, scr):
        own, other, prod, inv_v, sem_l, sem_s, sem_r = scr
        me, bits = my_bits()
        core = bits[0]
        shard, inv, block = refs[self.name + ":shard"], refs[self.name + ":inv"], refs[self.name + ":block"]
        load = pltpu.make_async_copy(shard, own, sem_l.at[0])
        inv_load = pltpu.make_async_copy(inv.at[block, :, pl.ds(pl.multiple_of(core * 768, 128), 768)], inv_v, sem_l.at[1])
        swap = pltpu.make_async_remote_copy(src_ref=shard, dst_ref=other, send_sem=sem_s.at[0], recv_sem=sem_r.at[0],
                                            device_id=(me + 1 - 2 * core,), device_id_type=MESH)

        def begin():
            load.start()
            swap.start()
            inv_load.start()

        def product():
            load.wait()
            inv_load.wait()
            swap.wait_recv()
            swap.wait_send()
            here = inv_v[pl.ds(pl.multiple_of(core * 768, 8), 768), :]
            there = inv_v[pl.ds(pl.multiple_of((1 - core) * 768, 8), 768), :]
            prod[...] = precise(own[...], here) + precise(other[...], there)

        return [begin, product]


class Fan(Job):
    def __init__(self, chain, row, dst, after):
        Job.__init__(self, "fan", chain, dst=dst)
        self.row, self.after = row, after


def precise(left, right):
    return lax.dot_general(left, right, NN, precision=lax.Precision.HIGHEST, preferred_element_type=f32)


def first_jobs(name):
    first = First(name)
    row, jobs = 0, [first]
    for chain in WIDE_CHAINS:
        jobs.append(Fan(chain, row, name + ":dst", first))
        row += 8
    return jobs


def rows_spec(tile):
    return pl.BlockSpec((tile, D), lambda i: (i, 0))


def cols_spec(height, tile):
    return pl.BlockSpec((height, tile), lambda i: (0, i))


def whole_spec(shape):
    zeros = (0,) * len(shape)
    return pl.BlockSpec(shape, lambda i: zeros, pipeline_mode=pl.Buffered(1))


def block_spec(shape, b):
    return pl.BlockSpec((1,) + shape[1:], lambda i: (b, 0, 0), pipeline_mode=pl.Buffered(1))


ANY = pl.BlockSpec(memory_space=pl.ANY)


def run_stage(body, name, tile, steps, ins, outs, scratch, jobs, extra, comm_ins, comm_outs, tick_us, flops, cid):
    def spec(kind, shape):
        if kind == "r":
            return rows_spec(tile)
        if kind == "c":
            return cols_spec(shape[0], tile)
        if kind == "w":
            return whole_spec(shape)
        return block_spec(shape, kind)

    slots, rest, end = plan(jobs, steps, tick_us)
    if DEBUG:
        print(name, "planned end", end, "compute", steps * tick_us, "rest", len(rest))
    scr = [job.scratch() for job in jobs]
    n_in, n_cin, n_out, n_cout, n_scr = len(ins), len(comm_ins), len(outs), len(comm_outs), len(scratch)

    def kernel(*refs):
        refs = list(refs)
        take = lambda n: [refs.pop(0) for _ in range(n)]
        c_in, m_in, c_out, m_out, c_scr = take(n_in), take(n_cin), take(n_out), take(n_cout), take(n_scr)
        named = dict(extra)
        named.update(zip(comm_ins, m_in))
        named.update(zip(comm_outs, m_out))
        step = pl.program_id(0)
        events = []
        if jobs:
            pl.when(step == 0)(entry_barrier)
            for job, s in zip(jobs, scr):
                mine = take(len(s))
                if job.kind == "first":
                    job.prod = mine[2]
                events.append(job.bind(named, mine))
        for t in range(steps):
            if slots[t]:
                @pl.when(step == t)
                def _(t=t):
                    for j, e in slots[t]:
                        events[j][e]()
        if body is not None:
            body(*c_in, *c_out, *c_scr)
        if rest:
            @pl.when(step == steps - 1)
            def _():
                for j, e in rest:
                    events[j][e]()

    params = dict(vmem_limit_bytes=63 * MIB)
    if jobs:
        params.update(collective_id=cid, has_side_effects=True)
    outputs = pl.pallas_call(
        kernel, grid=(steps,),
        in_specs=[spec(kind, arr.shape) for arr, kind in ins] + [ANY] * n_cin,
        out_specs=[spec(kind, shape) for shape, dtype, kind in outs] + [ANY] * n_cout,
        out_shape=[jax.ShapeDtypeStruct(shape, dtype) for shape, dtype, kind in outs]
        + [jax.ShapeDtypeStruct(shape, f32) for shape in comm_outs.values()],
        scratch_shapes=list(scratch) + [x for s in scr for x in s],
        compiler_params=pltpu.CompilerParams(**params),
        cost_estimate=pl.CostEstimate(flops=flops, bytes_accessed=40 * MIB, transcendentals=0),
        name=name)(*[arr for arr, _ in ins], *comm_ins.values())
    return outputs[:n_out], dict(zip(comm_outs, outputs[n_out:]))


DEBUG = False


def final_kernel(decay, t0, t1, t2, t3, old_s, old_a, s0, s1, s2, s3, old_u, old_q, n0, n1, n2, n3, inv_u, inv_q,
                 new_s, new_a, new_u, new_q, p_up, p_down, pk, od, nw, tr, sem_in, sem_out):
    rho = decay[0]
    scale = (1.0 - rho) * decay[1]
    units = []
    for src, old, new, b in ((t0, old_a, new_a, 0), (t1, old_a, new_a, 1), (t2, old_s, new_s, 0), (t3, old_s, new_s, 1)):
        off = 0
        for j in range(NB):
            units.append((src, old, new, b, j, off))
            off += (j + 1) * B

    def loads(u):
        src, old, new, b, j, off = units[u]
        rows, s = (j + 1) * B, u % 3
        return (pltpu.make_async_copy(src.at[pl.ds(off, rows), :], pk.at[s, pl.ds(0, rows), :], sem_in.at[s, 0]),
                pltpu.make_async_copy(old.at[b, pl.ds(0, rows), pl.ds(j * B, B)], od.at[s, pl.ds(0, rows), :], sem_in.at[s, 1]))

    def stores(u):
        src, old, new, b, j, off = units[u]
        rows, s = (j + 1) * B, u % 3
        ops = [pltpu.make_async_copy(nw.at[s, pl.ds(0, rows), :], new.at[b, pl.ds(0, rows), pl.ds(j * B, B)], sem_out.at[s, 0])]
        if j:
            ops.append(pltpu.make_async_copy(tr.at[s, :, pl.ds(0, j * B)], new.at[b, pl.ds(j * B, B), pl.ds(0, j * B)], sem_out.at[s, 1]))
        return ops

    def small(acc, old, new, b):
        top = rho * old[b, 0:128, :] + scale * acc[0]
        mid = rho * old[b, 128:256, 128:384] + scale * acc[1, :, 0:256]
        low = rho * old[b, 256:384, 256:384] + scale * acc[1, :, 256:384]
        new[b, 0:128, :] = top
        new[b, 128:256, 128:384] = mid
        new[b, 256:384, 256:384] = low
        new[b, 128:384, 0:128] = top[:, 128:384].T
        new[b, 256:384, 128:256] = mid[:, 128:256].T

    def up(n, b, h):
        p_up[b, :, h * 768:(h + 1) * 768] = precise(inv_u[b], n[h]) * decay[1]

    def down(n, b, h):
        p_down[b, h * 768:(h + 1) * 768, :] = precise(n[h].T, inv_q[b]) * decay[1]

    side = [functools.partial(small, *a) for a in
            ((s0, old_u, new_u, 0), (s1, old_u, new_u, 1), (s2, old_q, new_q, 0), (s3, old_q, new_q, 1))]
    for n, b, f in ((n0, 0, up), (n1, 1, up), (n2, 0, down), (n3, 1, down)):
        for h in range(2):
            side.append(functools.partial(f, n, b, h))
    for u in (0, 1):
        for c in loads(u):
            c.start()
    for u, (src, old, new, b, j, off) in enumerate(units):
        s = u % 3
        if u % 2 == 0:
            side[u // 2]()
        if u >= 3:
            for c in stores(u - 3):
                c.wait()
        for c in loads(u):
            c.wait()
        for i in range(j + 1):
            part = rho * od[s, i * B:(i + 1) * B, :] + scale * pk[s, i * B:(i + 1) * B, :]
            nw[s, i * B:(i + 1) * B, :] = part
            if i < j:
                tr[s, :, i * B:(i + 1) * B] = part.T
        for c in stores(u):
            c.start()
        if u + 2 < len(units):
            for c in loads(u + 2):
                c.start()
    for u in range(len(units) - 3, len(units)):
        for c in stores(u):
            c.wait()


def finish(decay, tris, smalls, prods, s_up_old, a_down_old, a_up_old, s_down_old, inv_u, inv_q):
    vmem = pl.BlockSpec(memory_space=pltpu.VMEM)
    big = jax.ShapeDtypeStruct(s_up_old.shape, f32)
    small = jax.ShapeDtypeStruct(a_up_old.shape, f32)
    return pl.pallas_call(
        final_kernel,
        in_specs=[pl.BlockSpec(memory_space=pltpu.SMEM)] + [ANY] * 6 + [vmem] * 12,
        out_specs=[ANY] * 2 + [vmem] * 4,
        out_shape=[big, big, small, small, jax.ShapeDtypeStruct((2, D, FF), f32), jax.ShapeDtypeStruct((2, FF, D), f32)],
        scratch_shapes=[pltpu.VMEM((3, FF, B), f32), pltpu.VMEM((3, FF, B), f32), pltpu.VMEM((3, FF, B), f32),
                        pltpu.VMEM((3, B, FF), f32), pltpu.SemaphoreType.DMA((3, 2)), pltpu.SemaphoreType.DMA((3, 2))],
        compiler_params=pltpu.CompilerParams(vmem_limit_bytes=63 * MIB),
        name="finish")(decay, *[t.reshape(TRI, B) for t in tris], s_up_old, a_down_old, *smalls, a_up_old, s_down_old,
                       *prods, inv_u, inv_q)


def solution(mesh):
    axis_size = mesh.shape["data"]
    tile = 512

    def local_step(tok, grad, w_up, w_down, a_up_old, s_up_old, a_down_old, s_down_old,
                   a_up_inv, s_up_inv, a_down_inv, s_down_inv, factor_decay):
        total = tok.shape[0]
        steps = total // tile
        inv_n = 1.0 / (total * axis_size)
        acts = pltpu.VMEM((FF, tile), bf16)
        w_t = pltpu.VMEM((FF, D), bf16)
        unit = 2 * total * FF * D
        shard = {"tri": (TRI // 32, B), "wide": (24, 768), "small": (8, 384)}

        def comm(rs=(), ag=(), ar=(), first=()):
            jobs, c_ins, c_outs, extra = [], {}, {}, {}
            for name, form, arr in ar:
                jobs += form_jobs("ar", form, name)
                c_ins[name + ":src"] = arr.reshape(FORMS[form][0])
                c_outs[name + ":dst"] = FORMS[form][0]
            for name, arr, inverse, block in first:
                jobs += first_jobs(name)
                c_ins[name + ":shard"] = arr
                c_ins[name + ":inv"] = inverse
                c_outs[name + ":dst"] = WIDE
                extra[name + ":block"] = block
            for name, form, arr in ag:
                jobs += form_jobs("ag", form, name)
                c_ins[name + ":shard"] = arr
                c_outs[name + ":dst"] = FORMS[form][0]
            for name, form, arr in rs:
                jobs += form_jobs("rs", form, name)
                c_ins[name + ":src"] = arr.reshape(FORMS[form][0])
                c_outs[name + ":shard"] = shard[form]
            return jobs, extra, c_ins, c_outs

        (pre0, u1, ad0, au0, sd1), _ = run_stage(
            stage1, "stage1", tile, steps, ((tok, "r"), (grad, "r"), (w_up, 0), (w_down, 0)),
            (((FF, total), bf16, "c"), ((D, total), bf16, "c"), ((TRI, B), f32, "w"), (SMALL, f32, "w"), (SMALL, f32, "w")),
            [acts, w_t, pltpu.VMEM((D, FF), bf16)], *comm(), 4.0, 5 * unit, 0)
        (pre1, ad1, au1, dwd1), c2 = run_stage(
            stage2, "stage2", tile, steps, ((u1, "c"), (grad, "r"), (w_up, 1)),
            (((FF, total), bf16, "c"), ((TRI, B), f32, "w"), (SMALL, f32, "w"), (WIDE, f32, "w")),
            [acts, w_t], *comm(rs=(("ad0", "tri", ad0), ("au0", "small", au0), ("sd1", "small", sd1))),
            3.8, 5 * unit, 1)
        (e1, su1, dwu1), c3 = run_stage(
            stage3, "stage3", tile, steps, ((pre1, "c"), (grad, "r"), (u1, "c"), (w_down, 1), (w_up, 1)),
            (((D, total), bf16, "c"), ((TRI, B), f32, "w"), (WIDE, f32, "w")),
            [acts], *comm(rs=(("ad1", "tri", ad1), ("au1", "small", au1), ("dwd1", "wide", dwd1)),
                          ag=(("ad0", "tri", c2["ad0:shard"]), ("au0", "small", c2["au0:shard"]), ("sd1", "small", c2["sd1:shard"]))),
            5.0, 6 * unit, 2)
        (g0, sd0, dwd0, dwu0), c4 = run_stage(
            stage4, "stage4", tile, steps, ((pre0, "c"), (tok, "r"), (e1, "c"), (w_down, 0)),
            (((FF, total), bf16, "c"), (SMALL, f32, "w"), (WIDE, f32, "w"), (WIDE, f32, "w")),
            [acts], *comm(rs=(("su1", "tri", su1), ("dwu1", "wide", dwu1)),
                          ag=(("ad1", "tri", c3["ad1:shard"]), ("au1", "small", c3["au1:shard"])),
                          first=(("dwd1", c3["dwd1:shard"], a_down_inv, 1),)),
            3.5, 4 * unit, 3)
        (su0,), c5 = run_stage(
            stage5, "stage5", tile, steps, ((g0, "c"),), (((TRI, B), f32, "w"),),
            [], *comm(rs=(("sd0", "small", sd0), ("dwd0", "wide", dwd0), ("dwu0", "wide", dwu0)),
                      ag=(("su1", "tri", c4["su1:shard"]),),
                      first=(("dwu1", c4["dwu1:shard"], s_up_inv, 1),)),
            1.8, 3 * unit, 4)
        _, c6 = run_stage(
            None, "tail", tile, 1, (), (), [],
            *comm(ar=(("su0", "tri", su0),), ag=(("sd0", "small", c5["sd0:shard"]),),
                  first=(("dwd0", c5["dwd0:shard"], a_down_inv, 0), ("dwu0", c5["dwu0:shard"], s_up_inv, 0))),
            0.1, unit, 5)
        decay = jnp.stack((factor_decay, jnp.float32(inv_n)))
        new_s, new_a, new_u, new_q, p_up, p_down = finish(
            decay, (c3["ad0:dst"], c4["ad1:dst"], c6["su0:dst"], c5["su1:dst"]),
            (c3["au0:dst"], c4["au1:dst"], c6["sd0:dst"], c3["sd1:dst"]),
            (c6["dwu0:dst"], c5["dwu1:dst"], c6["dwd0:dst"], c4["dwd1:dst"]),
            s_up_old, a_down_old, a_up_old, s_down_old, a_up_inv, s_down_inv)
        return p_up, p_down, new_u, new_s, new_a, new_q

    batch_spec = P("data", None)
    replicated = P()
    return jax.shard_map(local_step, mesh=mesh, in_specs=(batch_spec, batch_spec) + (replicated,) * 11,
                         out_specs=(replicated,) * 6, check_vma=False)
```

time: 1420 us -> 559 us (0.39)
  waiting for transfers between devices: 714 us -> 0 us
  matrix products: 581 us -> 0 us
  Pallas kernels: 0 us -> 549 us
  other arithmetic: 100 us -> 0.61 us
    psum x1 -> x0, waiting for transfers between devices: 714 us -> none  [local_step(): totals = [lax.psum(part, 'data') for part in local_parts]]
    dot_general x22 -> x0, matrix products: 581 us -> none  [the longest x12 316 us: cross_sum(): jnp.einsum('ti,tj->ij', left, right, preferred_element_type=jnp.float32)]
    pallas_call x0 -> x7, Pallas kernels: none -> 549 us  [the longest x6 486 us: run_stage(): pl.pallas_call(kernel, grid=(steps,), in_specs=[spec(kind, arr.shape) for...]
    add x2 -> x0, other arithmetic: 41.8 us -> none  [update_outputs(): factor_decay * old_part + (1.0 - factor_decay) * new_part]
    div x6 -> x0, other arithmetic: 32.2 us -> none  [stacked_sums(): jnp.stack([cross_sum(left, right) for left, right in zip(left_list, right...]
    dot_general x1 -> x0, other arithmetic: 26.2 us -> none  [cross_sum(): jnp.einsum('ti,tj->ij', left, right, preferred_element_type=jnp.float32)]
  transfers between devices with their start and end apart: 1 -> 0, of which waited for: 1 -> 0; matrix products, arithmetic and copies ran while one was open for 0% -> 0% of each run, Pallas kernels for 0% -> 0%
where the time goes in v1:
time: 559 us; the launch traced here: 552 us
  Pallas kernels  549 us (98%)
    pallas_call x6, Pallas kernels, run_stage(): pl.pallas_call(kernel, grid=(steps,), in_specs=[spec(kind, arr.shape) for...  486 us
    pallas_call x1, Pallas kernels, finish(): pl.pallas_call(final_kernel, in_specs=[pl.BlockSpec(memory_space=pltpu.SM...  63.3 us

profile of v1, /device:TPU:0, one launch (start us, length us, event | category | flops | bytes accessed | tf_op | source)
XLA Modules:
  0.0 551.7 jit_solution(3601574911661088406)
XLA Ops:
  0.6 67.3 %stage1.1 = (bf16[1536,8192]{1,0:T(8,128)(2,1)}, bf16[384,8192]{1,0:T(8,128)(2,1)}, f32[5376,256]{1,0:T(8,128)}, f32[2,128,384]{2,1,0:T(8,128)}, f32[2,128,384]{2,1,0:T(8,128)}) custom-call(bf16[8192,384]{1,0:T(8,128)(2,1)} %refs_1_.7, bf16[8192,384]{1,0:T(8,128)(2,1)} %refs_1_.6, bf16[2,384,1536]{2,1,0:T(8,128)(2,1)} %refs_4_.2, bf16[2,1536,384]{2,1,0:T(8,128)(2,1)} %refs_3_.5), custom_call_target="tpu_custom_call" | custom-call | flops 48318382080 | bytes 41943040 | tf_op jit(solution)/shard_map/stage1/pallas_call | solution.py:506
  68.0 69.6 %stage2.1 = (bf16[1536,8192]{1,0:T(8,128)(2,1)}, f32[5376,256]{1,0:T(8,128)}, f32[2,128,384]{2,1,0:T(8,128)}, f32[2,384,768]{2,1,0:T(8,128)}, f32[168,256]{1,0:T...) custom-call(bf16[384,8192]{1,0:T(8,128)(2,1)} %get-tuple-element.52.refs_0_.refs_2_, bf16[8192,384]{1,0:T(8,128)(2,1)} %refs_1_.6, ...), custom_call_target="tpu_custom_call" | custom-call | flops 48318382080 | bytes 41943040 | tf_op jit(solution)/shard_map/stage2/pallas_call | solution.py:506
  137.6 94.4 %stage3.1 = (bf16[384,8192]{1,0:T(8,128)(2,1)}, f32[5376,256]{1,0:T(8,128)}, f32[2,384,768]{2,1,0:T(8,128)}, f32[2,2688,256]{2,1,0:T(8,128)}, f32[2,128,384]{2,1...) custom-call(bf16[1536,8192]{1,0:T(8,128)(2,1)} %get-tuple-element.56.refs_0_, ...), custom_call_target="tpu_custom_call" | custom-call | flops 57982058496 | bytes 41943040 | tf_op jit(solution)/shard_map/stage3/pallas_call | solution.py:506
  232.0 88.3 %stage4.1 = (bf16[1536,8192]{1,0:T(8,128)(2,1)}, f32[2,128,384]{2,1,0:T(8,128)}, f32[2,384,768]{2,1,0:T(8,128)}, f32[2,384,768]{2,1,0:T(8,128)}, f32[2,384,768]{...) custom-call(bf16[1536,8192]{1,0:T(8,128)(2,1)} %get-tuple-element.64., ...), custom_call_target="tpu_custom_call" | custom-call | flops 38654705664 | bytes 41943040 | tf_op jit(solution)/shard_map/stage4/pallas_call | solution.py:506
  320.3 76.1 %stage5.1 = (f32[5376,256]{1,0:T(8,128)}, f32[2,384,768]{2,1,0:T(8,128)}, f32[2,2688,256]{2,1,0:T(8,128)}, f32[8,384]{1,0:T(8,128)}, f32[24,768]{1,0:T(8,128)}, /*index=5*/f32[24,768]{1,0:T(8,128)}) custom-call(bf16[1536,8192]{1,0:T(8,128)(2,1)} %get-tuple-element.72.refs_0_, f32[24,768]{1,0:T(8,128)} %get-tuple-element.73.refs_1_, ...), custom_call_target="tpu_custom_call" | custom-call | flops 28991029248 | bytes 41943040 | tf_op jit(solution)/shard_map/stage5/pallas_call | solution.py:506
  396.4 90.3 %tail.1 = (f32[2,2688,256]{2,1,0:T(8,128)}, f32[2,384,768]{2,1,0:T(8,128)}, f32[2,384,768]{2,1,0:T(8,128)}, f32[2,128,384]{2,1,0:T(8,128)}) custom-call(f32[2,2688,256]{2,1,0:T(8,128)} %bitcast.14, f32[24,768]{1,0:T(8,128)} %get-tuple-element.79.refs_1_, f32[2,1536,1536]{2,1,0:T(8,128)} %refs_2_.7, f32[24,768]{1,0:T(8,128)} %get-tuple-element.80.refs_3_, ...), custom_call_target="tpu_custom_call" | custom-call | flops 9663676416 | bytes 41943040 | tf_op jit(solution)/shard_map/tail/pallas_call | solution.py:506
  487.3 0.6 pad_maximum_fusion.decay
  487.9 63.3 %finish.1 = (f32[2,1536,1536]{2,1,0:T(8,128)}, f32[2,1536,1536]{2,1,0:T(8,128)}, f32[2,384,384]{2,1,0:T(8,128)}, f32[2,384,384]{2,1,0:T(8,128)}, f32[2,384,1536]{2,1,0:T(8,128)}, /*index=5*/f32[2,1536,384]{2,1,0:T(8,128)}) custom-call(f32[2]{0:T(128)} %pad_maximum_fusion.decay, f32[5376,256]{1,0:T(8,128)} %bitcast.10, f32[5376,256]{1,0:T(8,128)} %bitcast.11, ...), custom_call_target="tpu_custom_call" | custom-call | tf_op jit(solution)/shard_map/finish/pallas_call | solution.py:599
